TPU v7x, 128 devices: a whole 4x4x4 slice. The times are simulated.
128 devices in a mesh: cp: 32 (over x, y, core), tp: 4 (over z).
Axes of the slice: x: 4, y: 4, z: 4, core: 2. Of those that a mesh axis runs over, the one named last changes fastest.
Arguments:
- hidden: bfloat16 [8192, 4096], P('cp', 'tp'), may hold values from -120 to 120
- query_weight: bfloat16 [4096, 4096], P(None, 'tp'), may hold values from -0.1875 to 0.1875
- key_matrix: bfloat16 [4096, 512], P(None, 'tp'), may hold values from -0.09375 to 0.09375
- value_matrix: bfloat16 [4096, 512], P(None, 'tp'), may hold values from -0.09375 to 0.09375
- output_weight: bfloat16 [4096, 4096], P('tp'), may hold values from -0.1875 to 0.1875
- document_bounds: int32 [9], replicated, may hold values from 0 to 8192, as said below
- block_owner: int32 [64], replicated, may hold values from 0 to 31, as said below
Outputs:
- attended: bfloat16 [8192, 4096], P('cp', 'tp')
Inputs may be any that keep to these rules, and one draw needn't show every extreme that they name: document_bounds[0] = 0, document_bounds[8] = 8192, strictly rising; document i holds the tokens from document_bounds[i] to document_bounds[i + 1] - 1. `block_owner`: every index of cp is named by exactly 2 blocks.
All inputs are finite; a program needn't handle non-finite values.
Results may differ from a plain program's by a relative error of at most 0.012.
The roundings to bfloat16 on the way count: a program that leaves them out, or rounds other values in their place, can miss the bound.
Values may be sent and summed in bfloat16 or wider, within the bound.
A program may use at most 128 MiB of HBM per device.

v0:
```python
import math
import jax
import jax.numpy as jnp
from jax import lax
from jax.sharding import PartitionSpec as P

HEAD_WIDTH = 128
BLOCK = 128
rope_theta = 500000.0
rope_factor = 8.0
rope_context = 8192.0
masked_score = -1e30


def in_one_piece(arrays, axis, dim, along):
    both = jnp.concatenate(arrays, axis=along)
    filled, at, outs = (lax.all_gather(both, axis, axis=dim, tiled=True), 0, [])
    for a in arrays:
        outs.append(lax.slice_in_dim(filled, at, at + a.shape[along], axis=along))
        at += a.shape[along]
    return tuple(outs)


def rope_inverse(head_size):
    halves = jnp.arange(head_size // 2, dtype=jnp.float32)
    inverse = 1.0 / rope_theta ** (2.0 * halves / head_size)
    wavelength = 2.0 * math.pi / inverse
    smooth = (rope_context / wavelength - 1.0) / 3.0
    blended = (1.0 - smooth) * inverse / rope_factor + smooth * inverse
    longer = jnp.where(wavelength > rope_context, inverse / rope_factor, blended)
    return jnp.where(wavelength < rope_context / 4.0, inverse, longer)


def document_of(tokens, bounds):
    inner_bounds = bounds[1:-1]
    return jnp.sum((tokens[:, None] >= inner_bounds[None, :]).astype(jnp.int32), axis=1)


def position_of(tokens, bounds):
    starts = bounds[:-1]
    document_start = jnp.max(
        jnp.where(starts[None, :] <= tokens[:, None], starts[None, :], 0), axis=1
    )
    return tokens - document_start


def rotate(raw_rows, tokens, bounds, head_size):
    row_count = raw_rows.shape[0]
    head_count = raw_rows.shape[1] // head_size
    angles = (
        position_of(tokens, bounds).astype(jnp.float32)[:, None] * rope_inverse(head_size)[None, :]
    )
    cosine = jnp.cos(angles)[:, None, :]
    sine_table = jnp.sin(angles)[:, None, :]
    heads_view = raw_rows.reshape(row_count, head_count, head_size)
    front_half = heads_view[:, :, : head_size // 2]
    back_half = heads_view[:, :, head_size // 2 :]
    turned = jnp.concatenate(
        [
            front_half * cosine - back_half * sine_table,
            back_half * cosine + front_half * sine_table,
        ],
        axis=2,
    )
    return turned.reshape(row_count, head_count * head_size).astype(jnp.bfloat16)


def owner_order(block_owner, per_device):
    block_count = block_owner.shape[0]
    blocks = jnp.arange(block_count, dtype=jnp.int32)
    same_owner = block_owner[:, None] == block_owner[None, :]
    earlier = blocks[None, :] < blocks[:, None]
    owner_rank = jnp.sum((same_owner & earlier).astype(jnp.int32), axis=1)
    target = block_owner * per_device + owner_rank
    return jnp.sum(jnp.where(target[None, :] == blocks[:, None], blocks[None, :], 0), axis=1)


def relayout(local_rows, block_order):
    cp_size = lax.axis_size("cp")
    row_count, row_width = local_rows.shape
    per_device = row_count // BLOCK
    portion = BLOCK // cp_size
    pieces = local_rows.reshape(per_device, cp_size, portion * row_width)
    spread = lax.all_to_all(pieces, "cp", split_axis=1, concat_axis=0, tiled=True)
    spread = spread.reshape(per_device * cp_size, portion * row_width)
    wanted = block_order.reshape(cp_size, per_device).T.reshape(-1)
    outgoing = jnp.take(spread, wanted, axis=0).reshape(per_device, cp_size, portion * row_width)
    arrived = lax.all_to_all(outgoing, "cp", split_axis=1, concat_axis=1, tiled=True)
    return arrived.reshape(row_count, row_width)


def project(local_rows, query_weight, key_matrix, value_matrix):
    weight_list = (query_weight, key_matrix, value_matrix)
    portion = lax.all_gather(local_rows, "tp", axis=1, tiled=True)
    return tuple(
        (jnp.dot(portion, weight, preferred_element_type=jnp.float32) for weight in weight_list)
    )


def attend(queries, query_tokens, key_rows, value_rows, key_tokens, bounds, head_size, kv_heads):
    row_count = queries.shape[0]
    query_group_width = queries.shape[1] // (kv_heads * head_size)
    grouped = queries.reshape(row_count, kv_heads, query_group_width, head_size).transpose(
        1, 2, 0, 3
    )
    grouped = grouped.reshape(kv_heads, query_group_width * row_count, head_size)
    query_documents = document_of(query_tokens, bounds)
    score_scale = 1.0 / math.sqrt(head_size)

    def update(flash_state, key_block, value_block, token_block):
        block_rows = key_block.shape[0]
        key_documents = document_of(token_block, bounds)
        allowed = (query_documents[:, None] == key_documents[None, :]) & (
            token_block[None, :] <= query_tokens[:, None]
        )

        def compute(inner_state):
            running_max, running_sum, running_out = inner_state
            per_head_keys = key_block.reshape(block_rows, kv_heads, head_size).transpose(1, 0, 2)
            per_head_values = value_block.reshape(block_rows, kv_heads, head_size).transpose(
                1, 0, 2
            )
            scores = (
                jnp.einsum(
                    "khd,ksd->khs", grouped, per_head_keys, preferred_element_type=jnp.float32
                )
                * score_scale
            )
            wide_mask = jnp.tile(allowed, (query_group_width, 1))[None, :, :]
            scores = jnp.where(wide_mask, scores, masked_score)
            new_max = jnp.maximum(running_max, jnp.max(scores, axis=2))
            weights = jnp.where(wide_mask, jnp.exp(scores - new_max[:, :, None]), 0.0)
            factor = jnp.exp(running_max - new_max)
            new_sum = running_sum * factor + jnp.sum(weights, axis=2)
            new_out = running_out * factor[:, :, None] + jnp.einsum(
                "khs,ksd->khd",
                weights.astype(jnp.bfloat16),
                per_head_values,
                preferred_element_type=jnp.float32,
            )
            return (new_max, new_sum, new_out)

        return lax.cond(jnp.any(allowed), compute, lambda inner_state: inner_state, flash_state)

    initial = (
        jnp.full((kv_heads, query_group_width * row_count), masked_score, jnp.float32),
        jnp.zeros((kv_heads, query_group_width * row_count), jnp.float32),
        jnp.zeros((kv_heads, query_group_width * row_count, head_size), jnp.float32),
    )
    key_part, value_part, token_part = (
        *in_one_piece((key_rows, value_rows), "cp", 0, 1),
        lax.all_gather(key_tokens, "cp", axis=0, tiled=True),
    )
    part_rows = key_part.shape[0]
    block_rows = math.gcd(part_rows, 512)

    def one_block(block_index, inner_state):
        first_row = block_index * block_rows
        return update(
            inner_state,
            lax.dynamic_slice_in_dim(key_part, first_row, block_rows, 0),
            lax.dynamic_slice_in_dim(value_part, first_row, block_rows, 0),
            lax.dynamic_slice_in_dim(token_part, first_row, block_rows, 0),
        )

    final_max, final_sum, final_out = lax.fori_loop(0, part_rows // block_rows, one_block, initial)
    normalized = final_out / final_sum[:, :, None]
    merged = normalized.reshape(kv_heads, query_group_width, row_count, head_size).transpose(
        2, 0, 1, 3
    )
    return merged.reshape(row_count, kv_heads * query_group_width * head_size).astype(jnp.bfloat16)


def output_rows(heads_out, output_weight):
    head_terms = jnp.dot(heads_out, output_weight, preferred_element_type=jnp.float32)
    return lax.psum_scatter(head_terms.astype(jnp.bfloat16), "tp", scatter_dimension=1, tiled=True)


def local(
    hidden, query_weight, key_matrix, value_matrix, output_weight, document_bounds, block_owner
):
    cp_index = lax.axis_index("cp")
    row_count = hidden.shape[0]
    per_device = row_count // BLOCK
    block_order = owner_order(block_owner, per_device)
    own_blocks = lax.dynamic_slice_in_dim(block_order, cp_index * per_device, per_device, 0)
    new_tokens = (
        own_blocks[:, None] * BLOCK + jnp.arange(BLOCK, dtype=jnp.int32)[None, :]
    ).reshape(-1)
    kv_heads = key_matrix.shape[1] // HEAD_WIDTH
    query_raw, key_raw, value_raw = project(hidden, query_weight, key_matrix, value_matrix)
    key_tokens = cp_index * row_count + jnp.arange(row_count, dtype=jnp.int32)
    queries = relayout(rotate(query_raw, key_tokens, document_bounds, HEAD_WIDTH), block_order)
    key_rows = rotate(key_raw, key_tokens, document_bounds, HEAD_WIDTH)
    value_rows = value_raw.astype(jnp.bfloat16)
    heads_out = attend(
        queries, new_tokens, key_rows, value_rows, key_tokens, document_bounds, HEAD_WIDTH, kv_heads
    )
    return output_rows(heads_out, output_weight)


def solution(mesh):
    placed = (P("cp", "tp"), P(None, "tp"), P(None, "tp"), P(None, "tp"), P("tp", None), P(), P())
    return jax.shard_map(
        local, mesh=mesh, in_specs=placed, out_specs=P("cp", "tp"), check_vma=False
    )
```

profile of v0, /device:TPU:1, one launch (start us, length us, event | category | flops | bytes accessed | tf_op | source)
XLA Modules:
  0.0 271.1 jit_solution(13011074800097958751)
XLA Ops:
  8.1 35.0 %all-gather.4.cloned.1.call-done = bf16[256,4096]{1,0:T(8,128)(2,1)} async-done(((bf16[256,1024]{1,0:T(8,128)(2,1)}), bf16[256,4096]{1,0:T(8,128)(2,1)}) %all-gather.4.cloned.1.call-update) | async-done | bytes 2097168 | tf_op jit(solution)/shard_map/all_gather | solution.py:94
  43.1 2.6 convolution_bitcast_fusion.2
  46.0 2.7 convolution_convert_fusion.1
  50.5 5.7 %convolution_bitcast_fusion.1 = f32[32,8,8,128]{3,1,2,0:T(8,128)S(1)} fusion(bf16[256,4096]{1,0:T(8,128)(2,1)S(1)} %copy-done.1, bf16[4096,1024]{1,0:T(8,128)(2,1)} %param.12), kind=kOutput, calls=%fused_computation.28 | convolution fusion | flops 2147483648 | bytes 11534336 | tf_op jit(solution)/shard_map/dot_general | solution.py:96
  58.8 7.7 %all-to-all-start = ((bf16[2,32,4096]{2,0,1:T(2,128)(2,1)}), bf16[2,32,4096]{2,0,1:T(2,128)(2,1)S(1)}, u32[]{:S(2)}, u32[]{:S(2)}) async-start(bf16[2,32,4096]{2,0,1:T(2,128)(2,1)} %copy.48), calls=%async_computation | async-start | bytes 1048576 | tf_op jit(solution)/shard_map/all_to_all | solution.py:84
  66.6 11.5 %all-to-all-done = bf16[2,32,4096]{2,0,1:T(2,128)(2,1)S(1)} async-done(((bf16[2,32,4096]{2,0,1:T(2,128)(2,1)}), bf16[2,32,4096]{2,0,1:T(2,128)(2,1)S(1)}, u32[]{:S(2)}, u32[]{:S(2)}) %all-to-all-start) | async-done | bytes 524320 | tf_op jit(solution)/shard_map/all_to_all | solution.py:84
  80.7 4.0 %all-to-all-start.1 = ((bf16[2,32,4096]{2,0,1:T(2,128)(2,1)}), bf16[2,32,4096]{2,0,1:T(2,128)(2,1)S(1)}, u32[]{:S(2)}, u32[]{:S(2)}) async-start(bf16[2,32,4096]{2,0,1:T(2,128)(2,1)} %broadcast_select_fusion), calls=%async_computation.1 | async-start | bytes 1048576 | tf_op jit(solution)/shard_map/all_to_all | solution.py:88
  84.8 27.8 %all-gather = s32[32,1,256]{2,1,0:T(1,128)S(1)} all-gather(s32[1,1,256]{2,1,0:T(1,128)S(1)} %bitcast.88), channel_id=1, replica_groups=mesh['cp'=32,'tp'=4] {'cp'}, dimensions={0}, use_global_device_ids=true | all-gather | bytes 33792 | tf_op jit(solution)/shard_map/all_gather | solution.py:152
  114.2 3.9 %fusion.31 = (bf16[8192,128]{0,1:T(8,128)(2,1)}, bf16[8192,128]{0,1:T(8,128)(2,1)S(1)}) fusion(bf16[8192,256]{0,1:T(8,128)(2,1)} %all-gather.6.cloned.1.call-done), kind=kLoop, calls=%fused_computation.70 | loop fusion | bytes 8388608 | tf_op jit(solution)/shard_map/slice | solution.py:19
  118.1 4.1 %copy.54 = bf16[8192,128]{1,0:T(8,128)(2,1)} copy(bf16[8192,128]{0,1:T(8,128)(2,1)} %get-tuple-element.405) | data formatting | bytes 4194304
  122.2 2.4 copy.53
  124.8 63.4 %while.18 = (s32[]{:T(128)}, f32[1,2048]{1,0:T(1,128)S(1)}, f32[1,2048]{1,0:T(1,128)S(1)}, f32[1,2048,128]{2,1,0:T(8,128)S(1)}, s32[256]{0:T(256)S(1)}, /*index=...) while((s32[]{:T(128)}, f32[1,2048]{1,0:T(1,128)S(1)}, ...), condition=%wide.region_11.12_spmd.clone, body=%wide.region_4.11_spmd.clone.sunk | while | flops 551565568 | bytes 22167960 | solution.py:166
  138.7 7.1 %conditional.3 = ((f32[1,2048]{1,0:T(1,128)S(1)}, f32[1,2048]{1,0:T(1,128)S(1)}, f32[1,2048,128]{2,1,0:T(8,128)S(1)})) conditional(s32[]{:T(128)} %convert_element_type.86, (f32[1,2048]{1,0:T(1,128)S(1)}, f32[1,2048]{1,0:T(1,128)S(1)}, f32[1,2048,128]{2,1,0:T(8,128)S(1)}) %tuple.62, (pred[256,512]{0,1:T(8,128)(4,1)S(1)}, ...), branch_computations={%region_7.7_spmd, %region_8.10_spmd} | conditional | flops 551030784 | bytes 22021152 | solution.py:143
  143.1 2.7 fusion.5
  147.5 7.1 %conditional.3 = ((f32[1,2048]{1,0:T(1,128)S(1)}, f32[1,2048]{1,0:T(1,128)S(1)}, f32[1,2048,128]{2,1,0:T(8,128)S(1)})) conditional(s32[]{:T(128)} %convert_element_type.86, (f32[1,2048]{1,0:T(1,128)S(1)}, f32[1,2048]{1,0:T(1,128)S(1)}, f32[1,2048,128]{2,1,0:T(8,128)S(1)}) %tuple.62, (pred[256,512]{0,1:T(8,128)(4,1)S(1)}, ...), branch_computations={%region_7.7_spmd, %region_8.10_spmd} | conditional | flops 551030784 | bytes 22021152 | solution.py:143
  152.0 2.7 fusion.5
  156.4 7.1 %conditional.3 = ((f32[1,2048]{1,0:T(1,128)S(1)}, f32[1,2048]{1,0:T(1,128)S(1)}, f32[1,2048,128]{2,1,0:T(8,128)S(1)})) conditional(s32[]{:T(128)} %convert_element_type.86, (f32[1,2048]{1,0:T(1,128)S(1)}, f32[1,2048]{1,0:T(1,128)S(1)}, f32[1,2048,128]{2,1,0:T(8,128)S(1)}) %tuple.62, (pred[256,512]{0,1:T(8,128)(4,1)S(1)}, ...), branch_computations={%region_7.7_spmd, %region_8.10_spmd} | conditional | flops 551030784 | bytes 22021152 | solution.py:143
  160.8 2.7 fusion.5
  170.5 7.1 %conditional.3 = ((f32[1,2048]{1,0:T(1,128)S(1)}, f32[1,2048]{1,0:T(1,128)S(1)}, f32[1,2048,128]{2,1,0:T(8,128)S(1)})) conditional(s32[]{:T(128)} %convert_element_type.86, (f32[1,2048]{1,0:T(1,128)S(1)}, f32[1,2048]{1,0:T(1,128)S(1)}, f32[1,2048,128]{2,1,0:T(8,128)S(1)}) %tuple.62, (pred[256,512]{0,1:T(8,128)(4,1)S(1)}, ...), branch_computations={%region_7.7_spmd, %region_8.10_spmd} | conditional | flops 551030784 | bytes 22021152 | solution.py:143
  174.9 2.7 fusion.5
  179.3 7.1 %conditional.3 = ((f32[1,2048]{1,0:T(1,128)S(1)}, f32[1,2048]{1,0:T(1,128)S(1)}, f32[1,2048,128]{2,1,0:T(8,128)S(1)})) conditional(s32[]{:T(128)} %convert_element_type.86, (f32[1,2048]{1,0:T(1,128)S(1)}, f32[1,2048]{1,0:T(1,128)S(1)}, f32[1,2048,128]{2,1,0:T(8,128)S(1)}) %tuple.62, (pred[256,512]{0,1:T(8,128)(4,1)S(1)}, ...), branch_computations={%region_7.7_spmd, %region_8.10_spmd} | conditional | flops 551030784 | bytes 22021152 | solution.py:143
  183.7 2.7 fusion.5
  188.7 7.1 %convolution_convert_fusion = bf16[256,4096]{1,0:T(8,128)(2,1)} fusion(bf16[256,1024]{0,1:T(8,128)(2,1)S(1)} %bitcast.76, bf16[1024,4096]{1,0:T(8,128)(2,1)} %param.15), kind=kOutput, calls=%fused_computation.27 | convolution fusion | flops 2148532224 | bytes 11010048 | tf_op jit(solution)/shard_map/dot_general | solution.py:175
  195.9 68.7 %reduce-scatter.2.cloned.1.call-done = bf16[256,1024]{1,0:T(8,128)(2,1)} async-done(((bf16[256,4096]{1,0:T(8,128)(2,1)}), bf16[256,1024]{1,0:T(8,128)(2,1)}) %reduce-scatter.2.cloned.1.call-update) | async-done | bytes 524304 | tf_op jit(solution)/shard_map/reduce_scatter | solution.py:176
  (179 shorter events, 51.5 us)
Async XLA Ops:
  6.5 36.5 %copy-start = (bf16[4096,128]{1,0:T(8,128)(2,1)S(1)}, bf16[4096,128]{1,0:T(8,128)(2,1)}, u32[]{:S(2)}) copy-start(bf16[4096,128]{1,0:T(8,128)(2,1)} %param.13) | copy-start | bytes 3145732
  6.5 42.8 %copy-start.3 = (s32[64]{0:T(128)S(1)}, s32[64]{0:T(128)}, u32[]{:S(2)}) copy-start(s32[64]{0:T(128)} %param.17) | copy-start | bytes 772
  6.5 36.5 %all-gather.4.cloned.1.call-start = ((), (), s32[]{:S(2)}) async-start(), calls=%async_computation.3 | async-start | bytes 2621440 | tf_op jit(solution)/shard_map/all_gather | solution.py:94
  7.3 107.0 %all-gather.6.cloned.1.call-start = ((), (), s32[]{:S(2)}) async-start(), calls=%async_computation.4 | async-start | bytes 4325376 | tf_op jit(solution)/shard_map/all_gather | solution.py:17
  43.1 7.4 %copy-start.1 = (bf16[256,4096]{1,0:T(8,128)(2,1)S(1)}, bf16[256,4096]{1,0:T(8,128)(2,1)}, u32[]{:S(2)}) copy-start(bf16[256,4096]{1,0:T(8,128)(2,1)} %all-gather.4.cloned.1.call-done) | copy-start | bytes 6291460
  58.8 19.3 %all-to-all-start = ((bf16[2,32,4096]{2,0,1:T(2,128)(2,1)}), bf16[2,32,4096]{2,0,1:T(2,128)(2,1)S(1)}, u32[]{:S(2)}, u32[]{:S(2)}) async-start(bf16[2,32,4096]{2,0,1:T(2,128)(2,1)} %copy.48), calls=%async_computation | async-start | bytes 1048576 | tf_op jit(solution)/shard_map/all_to_all | solution.py:84
  66.5 18.2 %copy-start.2 = (s32[9]{0:T(128)S(1)}, s32[9]{0:T(128)}, u32[]{:S(2)}) copy-start(s32[9]{0:T(128)} %param.16) | copy-start | bytes 112
  80.7 32.1 %all-to-all-start.1 = ((bf16[2,32,4096]{2,0,1:T(2,128)(2,1)}), bf16[2,32,4096]{2,0,1:T(2,128)(2,1)S(1)}, u32[]{:S(2)}, u32[]{:S(2)}) async-start(bf16[2,32,4096]{2,0,1:T(2,128)(2,1)} %broadcast_select_fusion), calls=%async_computation.1 | async-start | bytes 1048576 | tf_op jit(solution)/shard_map/all_to_all | solution.py:88
  84.7 179.9 %reduce-scatter.2.cloned.1.call-start = ((), (), s32[]{:S(2)}) async-start(), calls=%async_computation.5 | async-start | bytes 2621440 | tf_op jit(solution)/shard_map/reduce_scatter | solution.py:176
Sparse Core Ops, SparseCore 0:
  9.0 34.0 all-gather.3
  49.5 56.5 all-gather.5
  196.0 68.4 reduce-scatter.1
where the time goes:
time: 272 us; the launch traced here: 271 us
  waiting for transfers between devices  116 us (43%)
  matrix products  41.3 us (15%)
  other arithmetic  27.8 us (10%)
  blocking collectives  27.8 us (10%)
  local copies, waits for them, and re-layouts  23.2 us (9%)
  between operations  13.3 us (5%)
  starting transfers between devices  11.8 us (4%)
  loops' own time  9.99 us (4%)
    reduce_scatter x1, waiting for transfers between devices, output_rows(): lax.psum_scatter(head_terms.astype(jnp.bfloat16), 'tp', scatter_dimension...  68.7 us
    all_gather x1, waiting for transfers between devices, project(): portion = lax.all_gather(local_rows, 'tp', axis=1, tiled=True)  35 us
    all_gather x1, blocking collectives, attend(): lax.all_gather(key_tokens, 'cp', axis=0, tiled=True)  27.8 us
    reduce_or x16, other arithmetic, update(): jnp.any(allowed)  13.3 us
    dot_general x5, matrix products, compute(): jnp.einsum('khs,ksd->khd', weights.astype(jnp.bfloat16), per_head_values,...  13.3 us
    all_to_all x1, waiting for transfers between devices, relayout(): lax.all_to_all(pieces, 'cp', split_axis=1, concat_axis=0, tiled=True)  11.5 us
    dot_general x3, matrix products, project(): jnp.dot(portion, weight, preferred_element_type=jnp.float32)  10.9 us
    dot_general x5, matrix products, compute(): jnp.einsum('khd,ksd->khs', grouped, per_head_keys, preferred_element_type...  9.97 us
  transfers between devices with their start and end apart: 5, of which 3 were waited for; matrix products, arithmetic and copies ran while one was open for 5% of the time, Pallas kernels for 0%

commit v1 on v0

--- a/solution.py
+++ b/solution.py
@@ -91,7 +91,8 @@
 
 def project(local_rows, query_weight, key_matrix, value_matrix):
     weight_list = (query_weight, key_matrix, value_matrix)
-    portion = lax.all_gather(local_rows, "tp", axis=1, tiled=True)
+    outgoing_2 = jnp.stack([local_rows] * lax.axis_size("tp"))
+    portion = jnp.concatenate(lax.all_to_all(outgoing_2, "tp", 0, 0), axis=1)
     return tuple(
         (jnp.dot(portion, weight, preferred_element_type=jnp.float32) for weight in weight_list)
     )

time: 272 us -> 286 us (1.051)
  local copies, waits for them, and re-layouts: 23.2 us -> 44.1 us
  waiting for transfers between devices: 116 us -> 108 us
  starting transfers between devices: 11.8 us -> 18.5 us
  matrix products: 41.3 us -> 38 us
    all_gather x1 -> x0, waiting for transfers between devices: 35 us -> none  [project(): portion = lax.all_gather(local_rows, 'tp', axis=1, tiled=True)]
    all_to_all x0 -> x1, waiting for transfers between devices: none -> 25.3 us  [project(): portion = jnp.concatenate(lax.all_to_all(outgoing_2, 'tp', 0, 0), axis=1)]
    dot_general x0 -> x1, local copies, waits for them, and re-layouts: none -> 11.3 us  [project(): jnp.dot(portion, weight, preferred_element_type=jnp.float32)]
    reshape x0 -> x3, local copies, waits for them, and re-layouts: none -> 6.42 us  [project(): portion = jnp.concatenate(lax.all_to_all(outgoing_2, 'tp', 0, 0), axis=1)]
    all_to_all x0 -> x1, starting transfers between devices: none -> 5.84 us  [project(): portion = jnp.concatenate(lax.all_to_all(outgoing_2, 'tp', 0, 0), axis=1)]
    dot_general x3, matrix products: 10.9 us -> 7.44 us  [project(): jnp.dot(portion, weight, preferred_element_type=jnp.float32)]
    unnamed x11 -> x12, local copies, waits for them, and re-layouts: 6.74 us -> 6.73 us
  transfers between devices with their start and end apart: 5 -> 5, of which waited for: 3 -> 3; matrix products, arithmetic and copies ran while one was open for 5% -> 11% of each run, Pallas kernels for 0% -> 0%
where the time goes in v1:
time: 286 us; the launch traced here: 284 us
  waiting for transfers between devices  108 us (38%)
  local copies, waits for them, and re-layouts  44.1 us (15%)
  matrix products  38 us (13%)
  other arithmetic  26.4 us (9%)
  blocking collectives  26.1 us (9%)
  starting transfers between devices  18.5 us (6%)
  between operations  13.7 us (5%)
  loops' own time  9.97 us (3%)
    reduce_scatter x1, waiting for transfers between devices, output_rows(): lax.psum_scatter(head_terms.astype(jnp.bfloat16), 'tp', scatter_dimension...  68.2 us
    all_gather x1, blocking collectives, attend(): lax.all_gather(key_tokens, 'cp', axis=0, tiled=True)  26.1 us
    all_to_all x1, waiting for transfers between devices, project(): portion = jnp.concatenate(lax.all_to_all(outgoing_2, 'tp', 0, 0), axis=1)  25.3 us
    all_to_all x1, waiting for transfers between devices, relayout(): lax.all_to_all(pieces, 'cp', split_axis=1, concat_axis=0, tiled=True)  14.3 us
    dot_general x5, matrix products, compute(): jnp.einsum('khs,ksd->khd', weights.astype(jnp.bfloat16), per_head_values,...  13.4 us
    reduce_or x16, other arithmetic, update(): jnp.any(allowed)  13.3 us
    dot_general x1, local copies, waits for them, and re-layouts, project(): jnp.dot(portion, weight, preferred_element_type=jnp.float32)  11.3 us
    dot_general x5, matrix products, compute(): jnp.einsum('khd,ksd->khs', grouped, per_head_keys, preferred_element_type...  10 us
  transfers between devices with their start and end apart: 5, of which 3 were waited for; matrix products, arithmetic and copies ran while one was open for 11% of the time, Pallas kernels for 0%

profile of v1, /device:TPU:1, one launch (start us, length us, event | category | flops | bytes accessed | tf_op | source)
XLA Modules:
  0.0 284.5 jit_solution(2724911203102471495)
XLA Ops:
  6.5 2.8 stack.2
  9.3 5.8 %all-to-all-start = ((bf16[4,256,1024]{2,1,0:T(8,128)(2,1)}), bf16[4,256,1024]{2,1,0:T(8,128)(2,1)S(1)}, u32[]{:S(2)}, u32[]{:S(2)}) async-start(bf16[4,256,1024]{2,1,0:T(8,128)(2,1)} %stack.2), calls=%async_computation | async-start | bytes 4194304 | tf_op jit(solution)/shard_map/all_to_all | solution.py:95
  15.3 25.3 %all-to-all-done = bf16[4,256,1024]{2,1,0:T(8,128)(2,1)S(1)} async-done(((bf16[4,256,1024]{2,1,0:T(8,128)(2,1)}), bf16[4,256,1024]{2,1,0:T(8,128)(2,1)S(1)}, u32[]{:S(2)}, u32[]{:S(2)}) %all-to-all-start) | async-done | bytes 2097184 | tf_op jit(solution)/shard_map/all_to_all | solution.py:95
  43.7 11.3 %copy.72 = bf16[1024,4096]{1,0:T(8,128)(2,1)} copy(bf16[1024,4096]{0,1:T(8,128)(2,1)} %bitcast.79) | data formatting | bytes 16777216 | tf_op jit(solution)/shard_map/dot_general | solution.py:97
  55.9 3.0 %copy.61 = bf16[256,4,1024]{2,1,0:T(4,128)(2,1)} copy(bf16[256,4,1024]{2,0,1:T(8,128)(2,1)S(1)} %bitcast.76) | data formatting | bytes 4194304 | tf_op jit(solution)/shard_map/reshape | solution.py:95
  58.9 3.3 %reshape.296 = bf16[256,4096,1]{1,0,2:T(8,128)(2,1)S(1)} reshape(bf16[256,4,1024]{2,1,0:T(4,128)(2,1)} %copy.61) | data formatting | bytes 4194304 | tf_op jit(solution)/shard_map/reshape | solution.py:95
  62.2 5.8 %fusion.32 = f32[256,8,128]{0,2,1:T(8,128)S(1)} fusion(bf16[256,4096,1]{1,0,2:T(8,128)(2,1)S(1)} %reshape.296, bf16[8,128,4096]{2,1,0:T(8,128)(2,1)} %bitcast.80), kind=kOutput, calls=%fused_computation.70 | convolution fusion | flops 2147483648 | bytes 11534336 | tf_op jit(solution)/shard_map/dot_general | solution.py:97
  70.0 8.9 %all-to-all-start.1 = ((bf16[2,32,4096]{2,0,1:T(2,128)(2,1)}), bf16[2,32,4096]{2,0,1:T(2,128)(2,1)S(1)}, u32[]{:S(2)}, u32[]{:S(2)}) async-start(bf16[2,32,4096]{2,0,1:T(2,128)(2,1)} %copy.64), calls=%async_computation.1 | async-start | bytes 1048576 | tf_op jit(solution)/shard_map/all_to_all | solution.py:84
  79.0 14.3 %all-to-all-done.1 = bf16[2,32,4096]{2,0,1:T(2,128)(2,1)S(1)} async-done(((bf16[2,32,4096]{2,0,1:T(2,128)(2,1)}), bf16[2,32,4096]{2,0,1:T(2,128)(2,1)S(1)}, u32[]{:S(2)}, u32[]{:S(2)}) %all-to-all-start.1) | async-done | bytes 524320 | tf_op jit(solution)/shard_map/all_to_all | solution.py:84
  95.8 3.7 %all-to-all-start.2 = ((bf16[2,32,4096]{2,0,1:T(2,128)(2,1)}), bf16[2,32,4096]{2,0,1:T(2,128)(2,1)S(1)}, u32[]{:S(2)}, u32[]{:S(2)}) async-start(bf16[2,32,4096]{2,0,1:T(2,128)(2,1)} %broadcast_select_fusion), calls=%async_computation.2 | async-start | bytes 1048576 | tf_op jit(solution)/shard_map/all_to_all | solution.py:88
  99.6 26.1 %all-gather = s32[32,1,256]{2,1,0:T(1,128)S(1)} all-gather(s32[1,1,256]{2,1,0:T(1,128)S(1)} %bitcast.95), channel_id=1, replica_groups=mesh['cp'=32,'tp'=4] {'cp'}, dimensions={0}, use_global_device_ids=true | all-gather | bytes 33792 | tf_op jit(solution)/shard_map/all_gather | solution.py:153
  127.4 3.9 %fusion.31 = (bf16[8192,128]{0,1:T(8,128)(2,1)S(1)}, bf16[8192,128]{0,1:T(8,128)(2,1)}) fusion(bf16[8192,256]{0,1:T(8,128)(2,1)} %all-gather.3.cloned.1.call-done), kind=kLoop, calls=%fused_computation.69 | loop fusion | bytes 8388608 | tf_op jit(solution)/shard_map/slice | solution.py:19
  131.3 4.1 %copy.69 = bf16[8192,128]{1,0:T(8,128)(2,1)} copy(bf16[8192,128]{0,1:T(8,128)(2,1)} %get-tuple-element.406) | data formatting | bytes 4194304
  137.9 63.7 %while.18 = (s32[]{:T(128)}, f32[1,2048]{1,0:T(1,128)S(1)}, f32[1,2048]{1,0:T(1,128)S(1)}, f32[1,2048,128]{2,1,0:T(8,128)S(1)}, s32[256]{0:T(256)S(1)}, /*index=...) while((s32[]{:T(128)}, f32[1,2048]{1,0:T(1,128)S(1)}, ...), condition=%wide.region_11.12_spmd.clone, body=%wide.region_4.11_spmd.clone.sunk | while | flops 551565568 | bytes 22167960 | solution.py:167
  151.9 7.2 %conditional.3 = ((f32[1,2048]{1,0:T(1,128)S(1)}, f32[1,2048]{1,0:T(1,128)S(1)}, f32[1,2048,128]{2,1,0:T(8,128)S(1)})) conditional(s32[]{:T(128)} %convert_element_type.86, (f32[1,2048]{1,0:T(1,128)S(1)}, f32[1,2048]{1,0:T(1,128)S(1)}, f32[1,2048,128]{2,1,0:T(8,128)S(1)}) %tuple.62, (pred[256,512]{0,1:T(8,128)(4,1)S(1)}, ...), branch_computations={%region_7.7_spmd, %region_8.10_spmd} | conditional | flops 551030784 | bytes 22021152 | solution.py:144
  156.4 2.7 fusion.5
  160.8 7.2 %conditional.3 = ((f32[1,2048]{1,0:T(1,128)S(1)}, f32[1,2048]{1,0:T(1,128)S(1)}, f32[1,2048,128]{2,1,0:T(8,128)S(1)})) conditional(s32[]{:T(128)} %convert_element_type.86, (f32[1,2048]{1,0:T(1,128)S(1)}, f32[1,2048]{1,0:T(1,128)S(1)}, f32[1,2048,128]{2,1,0:T(8,128)S(1)}) %tuple.62, (pred[256,512]{0,1:T(8,128)(4,1)S(1)}, ...), branch_computations={%region_7.7_spmd, %region_8.10_spmd} | conditional | flops 551030784 | bytes 22021152 | solution.py:144
  169.7 7.2 %conditional.3 = ((f32[1,2048]{1,0:T(1,128)S(1)}, f32[1,2048]{1,0:T(1,128)S(1)}, f32[1,2048,128]{2,1,0:T(8,128)S(1)})) conditional(s32[]{:T(128)} %convert_element_type.86, (f32[1,2048]{1,0:T(1,128)S(1)}, f32[1,2048]{1,0:T(1,128)S(1)}, f32[1,2048,128]{2,1,0:T(8,128)S(1)}) %tuple.62, (pred[256,512]{0,1:T(8,128)(4,1)S(1)}, ...), branch_computations={%region_7.7_spmd, %region_8.10_spmd} | conditional | flops 551030784 | bytes 22021152 | solution.py:144
  174.2 2.7 fusion.5
  183.8 7.2 %conditional.3 = ((f32[1,2048]{1,0:T(1,128)S(1)}, f32[1,2048]{1,0:T(1,128)S(1)}, f32[1,2048,128]{2,1,0:T(8,128)S(1)})) conditional(s32[]{:T(128)} %convert_element_type.86, (f32[1,2048]{1,0:T(1,128)S(1)}, f32[1,2048]{1,0:T(1,128)S(1)}, f32[1,2048,128]{2,1,0:T(8,128)S(1)}) %tuple.62, (pred[256,512]{0,1:T(8,128)(4,1)S(1)}, ...), branch_computations={%region_7.7_spmd, %region_8.10_spmd} | conditional | flops 551030784 | bytes 22021152 | solution.py:144
  188.3 2.7 fusion.5
  192.8 7.2 %conditional.3 = ((f32[1,2048]{1,0:T(1,128)S(1)}, f32[1,2048]{1,0:T(1,128)S(1)}, f32[1,2048,128]{2,1,0:T(8,128)S(1)})) conditional(s32[]{:T(128)} %convert_element_type.86, (f32[1,2048]{1,0:T(1,128)S(1)}, f32[1,2048]{1,0:T(1,128)S(1)}, f32[1,2048,128]{2,1,0:T(8,128)S(1)}) %tuple.62, (pred[256,512]{0,1:T(8,128)(4,1)S(1)}, ...), branch_computations={%region_7.7_spmd, %region_8.10_spmd} | conditional | flops 551030784 | bytes 22021152 | solution.py:144
  202.3 7.2 %convolution_convert_fusion = bf16[256,4096]{1,0:T(8,128)(2,1)} fusion(bf16[256,1024]{0,1:T(8,128)(2,1)S(1)} %bitcast.83, bf16[1024,4096]{1,0:T(8,128)(2,1)} %param.15), kind=kOutput, calls=%fused_computation.27 | convolution fusion | flops 2148532224 | bytes 11010048 | tf_op jit(solution)/shard_map/dot_general | solution.py:176
  209.5 68.2 %reduce-scatter.2.cloned.1.call-done = bf16[256,1024]{1,0:T(8,128)(2,1)} async-done(((bf16[256,4096]{1,0:T(8,128)(2,1)}), bf16[256,1024]{1,0:T(8,128)(2,1)}) %reduce-scatter.2.cloned.1.call-update) | async-done | bytes 524304 | tf_op jit(solution)/shard_map/reduce_scatter | solution.py:177
  (185 shorter events, 59.4 us)
Async XLA Ops:
  6.5 34.3 %copy-start = (bf16[4096,128]{1,0:T(8,128)(2,1)S(1)}, bf16[4096,128]{1,0:T(8,128)(2,1)}, u32[]{:S(2)}) copy-start(bf16[4096,128]{1,0:T(8,128)(2,1)} %param.13) | copy-start | bytes 3145732
  6.5 8.6 %copy-start.3 = (s32[9]{0:T(128)S(1)}, s32[9]{0:T(128)}, u32[]{:S(2)}) copy-start(s32[9]{0:T(128)} %param.16) | copy-start | bytes 112
  9.3 31.3 %all-to-all-start = ((bf16[4,256,1024]{2,1,0:T(8,128)(2,1)}), bf16[4,256,1024]{2,1,0:T(8,128)(2,1)S(1)}, u32[]{:S(2)}, u32[]{:S(2)}) async-start(bf16[4,256,1024]{2,1,0:T(8,128)(2,1)} %stack.2), calls=%async_computation | async-start | bytes 4194304 | tf_op jit(solution)/shard_map/all_to_all | solution.py:95
  15.1 112.3 %all-gather.3.cloned.1.call-start = ((), (), s32[]{:S(2)}) async-start(), calls=%async_computation.4 | async-start | bytes 4325376 | tf_op jit(solution)/shard_map/all_gather | solution.py:17
  40.6 1.2 copy-start.2
  43.7 11.3 %copy-start.4 = (s32[64]{0:T(128)S(1)}, s32[64]{0:T(128)}, u32[]{:S(2)}) copy-start(s32[64]{0:T(128)} %param.17) | copy-start | bytes 772
  70.0 23.2 %all-to-all-start.1 = ((bf16[2,32,4096]{2,0,1:T(2,128)(2,1)}), bf16[2,32,4096]{2,0,1:T(2,128)(2,1)S(1)}, u32[]{:S(2)}, u32[]{:S(2)}) async-start(bf16[2,32,4096]{2,0,1:T(2,128)(2,1)} %copy.64), calls=%async_computation.1 | async-start | bytes 1048576 | tf_op jit(solution)/shard_map/all_to_all | solution.py:84
  95.8 30.2 %all-to-all-start.2 = ((bf16[2,32,4096]{2,0,1:T(2,128)(2,1)}), bf16[2,32,4096]{2,0,1:T(2,128)(2,1)S(1)}, u32[]{:S(2)}, u32[]{:S(2)}) async-start(bf16[2,32,4096]{2,0,1:T(2,128)(2,1)} %broadcast_select_fusion), calls=%async_computation.2 | async-start | bytes 1048576 | tf_op jit(solution)/shard_map/all_to_all | solution.py:88
  99.5 178.2 %reduce-scatter.2.cloned.1.call-start = ((), (), s32[]{:S(2)}) async-start(), calls=%async_computation.5 | async-start | bytes 2621440 | tf_op jit(solution)/shard_map/reduce_scatter | solution.py:177
  202.3 75.4 %copy-start.1 = (bf16[4096,128]{1,0:T(8,128)(2,1)S(1)}, bf16[4096,128]{1,0:T(8,128)(2,1)}, u32[]{:S(2)}) copy-start(bf16[4096,128]{1,0:T(8,128)(2,1)} %param.13) | copy-start | bytes 3145732
Sparse Core Ops, SparseCore 0:
  43.8 54.7 all-gather.2
  209.6 68.0 reduce-scatter.1
